TPU v7x, 32 devices: a whole 2x2x4 slice. The times are simulated.
32 devices in a mesh: band: 8 (over z, core), lane: 4 (over y, x).
Axes of the slice: x: 2, y: 2, z: 4, core: 2. Of those that a mesh axis runs over, the one named last changes fastest.
Arguments:
- first_factor: bfloat16 [8192, 4096], P('band', 'lane'), may hold values from -6 to 6
- second_factor: bfloat16 [4096, 2048], P('band', 'lane'), may hold values from -0.09375 to 0.09375
- result_in: float32 [8192, 2048], P('band', 'lane'), may hold values from -6 to 6
- pivot_scale: float32 [4096], replicated, may hold values from 0.25 to 1.75
Outputs:
- updated: float32 [8192, 2048], P('band', 'lane')
All inputs are finite; a program needn't handle non-finite values.
Results may differ from a plain program's by a relative error of at most 0.002.
Values may be sent and summed in bfloat16 or wider, within the bound.
A program may use at most 128 MiB of HBM per device.

v0:
```python
import functools

import jax
import jax.numpy as jnp
from jax import lax
from jax.experimental import pallas as pl
from jax.experimental.pallas import tpu as pltpu
from jax.sharding import PartitionSpec as P

MESH = pl.DeviceIdType.MESH
PIECES = 4
TILES = 2


def gathered(first_factor, second_factor, result_in, pivot_scale):
    share = first_factor.shape[1]
    part_scale = lax.dynamic_slice_in_dim(pivot_scale, lax.axis_index("lane") * share, share)
    scaled_left = (first_factor.astype(jnp.float32) * part_scale).astype(jnp.bfloat16)
    left_line = lax.all_gather(scaled_left, "lane", axis=1, tiled=True)
    right = lax.all_gather(second_factor, "band", axis=0, tiled=True)
    updated = result_in - jnp.dot(left_line, right, preferred_element_type=jnp.float32)
    row_power = lax.psum(jnp.sum(updated * updated, axis=1), "lane")
    return (
        updated * lax.rsqrt(row_power / (updated.shape[1] * lax.axis_size("lane")) + 1e-06)[:, None]
    )


def kernel(
    chips, left_hbm, right_hbm, result_hbm, scale_ref, out_ref, power_ref,
    left_raw, left, right, result, outgoing, incoming, kept, norm_out, norm_in,
    load_sem, source_sem, right_sem, up_sem, down_sem, peer_send, peer_recv, part_send, part_recv,
    norm_send, norm_recv,
):
    band, lane = lax.axis_index("band"), lax.axis_index("lane")
    z, core = band // 2, band % 2
    y, x = lane // 2, lane % 2
    peer = (2 * z + 1 - core, lane)
    lane_x, lane_y, lane_d = 2 * y + 1 - x, 2 * (1 - y) + x, 2 * (1 - y) + 1 - x
    above, below = (band + 2, lane), (band - 2, lane)
    depth, width = right_hbm.shape
    half = width // 2
    piece = depth // PIECES
    rows, share = left.shape
    tile = rows // TILES

    load_left = pltpu.make_async_copy(left_hbm, left_raw, load_sem.at[0])
    load_left.start()
    load_result = pltpu.make_async_copy(result_hbm, result, load_sem.at[1])
    load_result.start()

    barrier = pltpu.get_barrier_semaphore()
    for other in (lane_x, lane_y, lane_d):
        pl.semaphore_signal(barrier, inc=1, device_id=(band, other), device_id_type=MESH)
    pl.semaphore_signal(barrier, inc=1, device_id=peer, device_id_type=MESH)

    @pl.when(z < chips - 1)
    def _():
        pl.semaphore_signal(barrier, inc=1, device_id=above, device_id_type=MESH)

    @pl.when(z > 0)
    def _():
        pl.semaphore_signal(barrier, inc=1, device_id=below, device_id_type=MESH)

    pl.semaphore_wait(barrier, 4 + (z + chips - 1) // chips + (2 * chips - 2 - z) // chips)

    def place(slot, part, of_core):
        start = pl.multiple_of(of_core * depth + part * piece, piece)
        return right.at[slot, pl.ds(start, piece), :]

    dx, dy = (x + z % 2) % 2, (y + z // 2) % 2
    slot_0 = dx * (1 - dy) + 6 * (1 - dx) * dy + 4 * dx * dy
    slot_1 = 7 * (1 - dx) * (1 - dy) + 5 * dx * (1 - dy) + 3 * (1 - dx) * dy + 2 * dx * dy

    def own_block(i, part):
        side = (i + dy) % 2
        slot = slot_0 * (1 - side) + slot_1 * side
        block = right_hbm.at[
            pl.ds(part * piece, piece), pl.ds(pl.multiple_of(side * half, half), half)
        ]
        return block, slot

    def send_own(i, part):
        block, slot = own_block(i, part)
        return pltpu.make_async_remote_copy(
            block, place(slot, part, core), source_sem.at[i * PIECES + part],
            right_sem.at[slot * PIECES + part], device_id=(band, z), device_id_type=MESH,
        )

    @pl.when(lane != z)
    def _():
        for i in range(2):
            for part in range(PIECES):
                send_own(i, part).start()

    @pl.when(lane == z)
    def _():
        for i in range(2):
            for part in range(PIECES):
                block, slot = own_block(i, part)
                pltpu.make_async_copy(
                    block, place(slot, part, core), right_sem.at[slot * PIECES + part]
                ).start()

    def along(slot, part, device, send, recv):
        at = slot * PIECES + part
        ref = place(slot, part, core)
        return pltpu.make_async_remote_copy(
            ref, ref, send.at[at], recv.at[at], device_id=device, device_id_type=MESH
        )

    def forward(slot):
        for part in range(PIECES):
            along(slot, part, peer, peer_send, right_sem).wait_recv()

            @pl.when((z >= lane) & (z < chips - 1))
            def _():
                along(slot, part, above, up_sem, right_sem).start()

            @pl.when((z <= lane) & (z > 0))
            def _():
                along(slot, part, below, down_sem, right_sem).start()

            along(slot, part, peer, peer_send, peer_recv).start()

    def await_peer(slot):
        for part in range(PIECES):
            at = slot * PIECES + part
            ref = place(slot, part, 1 - core)
            pltpu.make_async_remote_copy(
                ref, ref, peer_send.at[at], peer_recv.at[at], device_id=peer, device_id_type=MESH
            ).wait_recv()

    def part_copy(buffer, at, other):
        index = buffer * TILES + at
        span = pl.ds(pl.multiple_of(at * tile, tile), tile)
        return pltpu.make_async_remote_copy(
            outgoing.at[buffer, span, :], incoming.at[buffer, span, :], part_send.at[index],
            part_recv.at[index], device_id=(band, other), device_id_type=MESH,
        )

    def product(slot, span):
        return jnp.dot(left[span, :], right[slot], preferred_element_type=jnp.float32)

    def each_tile(body):
        @pl.loop(0, TILES)
        def _(at):
            body(at, pl.ds(pl.multiple_of(at * tile, tile), tile))

    def multiply_send(slot, buffer, other):
        def body(at, span):
            outgoing[buffer, span, :] = product(slot, span).astype(jnp.bfloat16)
            part_copy(buffer, at, other).start()

        each_tile(body)

    def multiply_keep(slot, which):
        def body(at, span):
            kept[which, span, :] = product(slot, span)

        each_tile(body)

    def combine_send(which, arrived, buffer, other):
        def body(at, span):
            part_copy(arrived, at, other).wait_recv()
            total = kept[which, span, :] + incoming[arrived, span, :].astype(jnp.float32)
            outgoing[buffer, span, :] = total.astype(jnp.bfloat16)
            part_copy(buffer, at, other).start()

        each_tile(body)

    def multiply_own(slot, side):
        def body(at, span):
            columns = slice(side * half, (side + 1) * half)
            out_ref[span, columns] = result[span, columns] - product(slot, span)

        each_tile(body)

    forward(0)
    load_left.wait()
    part_scale = scale_ref[:, pl.ds(pl.multiple_of(lane * share, share), share)]

    def scale_tile(at, span):
        left[span, :] = (left_raw[span, :].astype(jnp.float32) * part_scale).astype(jnp.bfloat16)

    each_tile(scale_tile)

    await_peer(0)
    load_result.wait()
    multiply_own(0, 0)
    forward(1)
    await_peer(1)
    multiply_send(1, 2, lane_x)
    forward(2)
    await_peer(2)
    multiply_send(2, 1, lane_y)
    forward(3)
    await_peer(3)
    multiply_send(3, 3, lane_y)
    forward(4)
    await_peer(4)
    multiply_send(4, 0, lane_x)
    forward(5)
    await_peer(5)
    multiply_keep(5, 0)
    forward(6)
    await_peer(6)
    multiply_keep(6, 1)
    combine_send(0, 1, 4, lane_x)
    combine_send(1, 0, 5, lane_y)
    forward(7)
    await_peer(7)
    multiply_own(7, 1)

    def finish(at, span):
        for buffer in (2, 3, 4, 5):
            part_copy(buffer, at, lane_x).wait_recv()
        first = out_ref[span, :half] - (
            incoming[2, span, :].astype(jnp.float32) + incoming[5, span, :].astype(jnp.float32)
        )
        second = out_ref[span, half:] - (
            incoming[3, span, :].astype(jnp.float32) + incoming[4, span, :].astype(jnp.float32)
        )
        out_ref[span, :half] = first
        out_ref[span, half:] = second
        power = first * first + second * second
        power = sum(power[:, k : k + 128] for k in range(0, half, 128))
        norm_out[:, span] = jnp.sum(power.T.reshape(16, 8, tile), axis=0)

    each_tile(finish)

    norms = [
        pltpu.make_async_remote_copy(
            norm_out, norm_in.at[k], norm_send.at[k], norm_recv.at[k],
            device_id=(band, other), device_id_type=MESH,
        )
        for k, other in enumerate((lane_x, lane_y, lane_d))
    ]
    for copy in norms:
        copy.start()

    @pl.when(lane != z)
    def _():
        for i in range(2):
            for part in range(PIECES):
                send_own(i, part).wait_send()

    for slot in range(8):
        for part in range(PIECES):
            along(slot, part, peer, peer_send, peer_recv).wait_send()

    @pl.when((z >= lane) & (z < chips - 1))
    def _():
        for slot in range(8):
            for part in range(PIECES):
                along(slot, part, above, up_sem, right_sem).wait_send()

    @pl.when((z <= lane) & (z > 0))
    def _():
        for slot in range(8):
            for part in range(PIECES):
                along(slot, part, below, down_sem, right_sem).wait_send()

    for buffer in range(6):
        for at in range(TILES):
            part_copy(buffer, at, lane_x).wait_send()

    for copy in norms:
        copy.wait()
    power = norm_out[...] + norm_in[0] + norm_in[1] + norm_in[2]
    power = jnp.sum(power, axis=0, keepdims=True)
    power_ref[...] = jnp.broadcast_to(power, (128, rows)).T


def on_device(chips, first_factor, second_factor, result_in, pivot_scale):
    rows, share = first_factor.shape
    depth, width = second_factor.shape
    half = width // 2
    slots = 8 * PIECES
    dma = pltpu.SemaphoreType.DMA
    flops = 2 * rows * share * 4 * width
    updated, power = pl.pallas_call(
        functools.partial(kernel, chips),
        out_shape=(
            jax.ShapeDtypeStruct((rows, width), jnp.float32),
            jax.ShapeDtypeStruct((rows, 128), jnp.float32),
        ),
        in_specs=[
            pl.BlockSpec(memory_space=pltpu.HBM),
            pl.BlockSpec(memory_space=pl.ANY),
            pl.BlockSpec(memory_space=pl.ANY),
            pl.BlockSpec(memory_space=pltpu.VMEM),
        ],
        out_specs=[pl.BlockSpec(memory_space=pltpu.VMEM)] * 2,
        scratch_shapes=[
            pltpu.VMEM((rows, share), jnp.bfloat16),
            pltpu.VMEM((rows, share), jnp.bfloat16),
            pltpu.VMEM((8, share, half), jnp.bfloat16),
            pltpu.VMEM((rows, width), jnp.float32),
            pltpu.VMEM((6, rows, half), jnp.bfloat16),
            pltpu.VMEM((6, rows, half), jnp.bfloat16),
            pltpu.VMEM((2, rows, half), jnp.float32),
            pltpu.VMEM((8, rows), jnp.float32),
            pltpu.VMEM((3, 8, rows), jnp.float32),
            dma((2,)),
            dma((2 * PIECES,)),
            dma((slots,)),
            dma((slots,)),
            dma((slots,)),
            dma((slots,)),
            dma((slots,)),
            dma((6 * TILES,)),
            dma((6 * TILES,)),
            dma((3,)),
            dma((3,)),
        ],
        compiler_params=pltpu.CompilerParams(
            collective_id=0, has_side_effects=True, vmem_limit_bytes=48 * 1024 * 1024
        ),
        cost_estimate=pl.CostEstimate(
            flops=flops, bytes_accessed=8 * rows * share, transcendentals=0
        ),
    )(first_factor, second_factor, result_in, pivot_scale.reshape(1, -1))
    return updated * lax.rsqrt(power[:, :1] / (width * lax.axis_size("lane")) + 1e-06)


def solution(mesh):
    bands, lanes = mesh.shape["band"], mesh.shape["lane"]

    def body(first_factor, second_factor, result_in, pivot_scale):
        fits = lanes == 4 and bands == 2 * lanes
        plan = functools.partial(on_device, bands // 2) if fits else gathered
        return plan(first_factor, second_factor, result_in, pivot_scale)

    return jax.shard_map(
        body,
        mesh=mesh,
        in_specs=(P("band", "lane"), P("band", "lane"), P("band", "lane"), P()),
        out_specs=P("band", "lane"),
        check_vma=False,
    )
```

profile of v0, /device:TPU:0, one launch (start us, length us, event | category | flops | bytes accessed | tf_op | source)
XLA Modules:
  0.0 80.5 jit_solution(17103007908420895798)
XLA Ops:
  0.0 0.0 copy-start
  0.0 1.6 %copy-done = bf16[1024,1024]{1,0:T(8,128)(2,1)S(1)} copy-done((bf16[1024,1024]{1,0:T(8,128)(2,1)S(1)}, bf16[1024,1024]{1,0:T(8,128)(2,1)}, u32[]{:S(2)}) %copy-start) | copy-done | bytes 2097176
  1.6 0.0 copy-start.1
  1.6 1.0 %copy-done.1 = bf16[512,512]{1,0:T(8,128)(2,1)S(1)} copy-done((bf16[512,512]{1,0:T(8,128)(2,1)S(1)}, bf16[512,512]{1,0:T(8,128)(2,1)}, u32[]{:S(2)}) %copy-start.1) | copy-done | bytes 524312
  2.6 0.0 copy-start.2
  2.6 0.7 copy-done.2
  3.4 75.4 %shard_map.46 = (f32[1024,512]{1,0:T(8,128)S(1)}, f32[1024,128]{1,0:T(8,128)S(1)}) custom-call(bf16[1024,1024]{1,0:T(8,128)(2,1)S(1)} %copy-done, bf16[512,512]{1,0:T(8,128)(2,1)S(1)} %copy-done.1, f32[1024,512]{1,0:T(8,128)} %result_hbm.1, f32[1,4096]{1,0:T(1,128)S(1)} %bitcast.1), custom_call_target="tpu_custom_call" | custom-call | flops 4294967296 | bytes 8388608 | tf_op jit(solution)/shard_map/pallas_call | solution.py:281
  78.8 0.2 rsqrt_reduce_fusion
  79.0 1.5 %broadcast_multiply_fusion = f32[1024,512]{1,0:T(8,128)} fusion(f32[1024,512]{1,0:T(8,128)S(1)} %get-tuple-element.7, f32[1024]{0:T(1024)S(1)} %rsqrt_reduce_fusion), kind=kLoop, calls=%fused_computation | loop fusion | flops 524288 | bytes 4198400 | tf_op jit(solution)/shard_map/mul | solution.py:323
Async XLA Ops:
  0.0 1.6 %copy-start = (bf16[1024,1024]{1,0:T(8,128)(2,1)S(1)}, bf16[1024,1024]{1,0:T(8,128)(2,1)}, u32[]{:S(2)}) copy-start(bf16[1024,1024]{1,0:T(8,128)(2,1)} %left_hbm.1) | copy-start | bytes 6291460
  1.6 1.0 %copy-start.1 = (bf16[512,512]{1,0:T(8,128)(2,1)S(1)}, bf16[512,512]{1,0:T(8,128)(2,1)}, u32[]{:S(2)}) copy-start(bf16[512,512]{1,0:T(8,128)(2,1)} %right_hbm.1) | copy-start | bytes 1572868
  2.6 0.7 copy-start.2
where the time goes:
time: 80.7 us; the launch traced here: 80.5 us
  Pallas kernels  75.4 us (93%)
  local copies, waits for them, and re-layouts  3.35 us (4%)
  other arithmetic  1.74 us (2%)
    pallas_call x1, Pallas kernels, on_device(): pl.pallas_call(functools.partial(kernel, chips), out_shape=(jax.ShapeDtyp...  75.4 us
    unnamed x6, local copies, waits for them, and re-layouts  3.35 us

commit v1 on v0

v1 whole, which is shorter than its diff:
```python
import functools

import jax
import jax.numpy as jnp
from jax import lax
from jax.experimental import pallas as pl
from jax.experimental.pallas import tpu as pltpu
from jax.sharding import PartitionSpec as P

MESH = pl.DeviceIdType.MESH
PIECES = 4
CHUNKS = 8
X0, X1, D0, D1 = 0, 1, 2, 3

FIRST = (
    (("-D", 0, "u"),),
    (("-D", 0, "ud"), ("-D", 1, "u")),
    (("-D", 0, "y"), ("-D", 1, "y"), ("-D", 2, "y"), ("-D", 3, "y")),
    (
        ("-D", 0, "dy"), ("-D", 1, "dy"), ("-D", 2, "dy"), ("-D", 3, "dy"),
    ),
)
STEPS = (
    (
        ((D0, 0, ""), (D0, 1, ""), (D0, 2, ""), (D0, 3, ""), (X0, 0, "u")),
        ((D1, 0, ""), (D1, 1, ""), (D1, 2, ""), (D1, 3, ""), (X1, 0, "ud")),
        (("H", 0, "d"), (D1, 0, "u"), (D1, 1, "u")),
        (),
    ),
    (
        ((X0, 1, "u"), (X1, 0, ""), (X0, 2, "u"), (X1, 1, "")),
        ((X1, 1, "ud"), ("H", 0, "dy"), (X1, 2, "u"), ("H", 1, "dy")),
        (("H", 1, "d"), (X1, 0, "u"), ("H", 2, "d")),
        ((D1, 0, ""), (D1, 1, "")),
    ),
    (
        ((X0, 3, "u"), ("-D", 1, "u"), ("-D", 2, "u"), ("-D", 3, "u"), ("H", 0, "y"), ("H", 1, "y")),
        (
            (X1, 3, "u"), ("-D", 2, "u"), ("-D", 3, "u"), ("H", 2, "dy"), ("H", 3, "dy"),
            ("-X1", 2, "d"), ("-X1", 3, "d"), ("-D", 1, "d"), ("-D", 2, "d"), ("-D", 3, "d"),
        ),
        ((X1, 1, "u"), ("H", 3, "d"), (X0, 0, ""), (X1, 2, "u"), (X0, 1, "")),
        ((X1, 0, ""), (X1, 1, "")),
    ),
    (
        (("H", 2, "y"), ("H", 3, "y"), (X1, 2, ""), (X1, 3, "")),
        ((X0, 0, ""), (X0, 1, ""), (X0, 2, ""), (X0, 3, ""), (D0, 0, "u"), (D0, 1, "u")),
        ((X1, 3, "u"), (X0, 2, ""), (X0, 3, ""), (D1, 2, "u")),
        ((X1, 2, ""), (X1, 3, ""), (X0, 0, ""), (X0, 1, ""), (X0, 2, ""), (X0, 3, "")),
    ),
    (
        ((D1, 0, ""), (D1, 1, "")),
        ((D0, 2, "u"), (D0, 3, "u")),
        ((D1, 3, "u"),),
        ((D1, 2, ""),),
    ),
    (
        ((D1, 2, ""),),
        (),
        ((D0, 0, "u"), (D0, 1, "u")),
        ((D1, 3, ""), (D0, 0, "")),
    ),
    (
        ((D1, 3, ""),),
        (),
        ((D0, 2, "u"), (D0, 3, "u")),
        ((D0, 1, ""), (D0, 2, ""), (D0, 3, "")),
    ),
)


def gathered(first_factor, second_factor, result_in, pivot_scale):
    share = first_factor.shape[1]
    part_scale = lax.dynamic_slice_in_dim(pivot_scale, lax.axis_index("lane") * share, share)
    scaled_left = (first_factor.astype(jnp.float32) * part_scale).astype(jnp.bfloat16)
    left_line = lax.all_gather(scaled_left, "lane", axis=1, tiled=True)
    right = lax.all_gather(second_factor, "band", axis=0, tiled=True)
    updated = result_in - jnp.dot(left_line, right, preferred_element_type=jnp.float32)
    row_power = lax.psum(jnp.sum(updated * updated, axis=1), "lane")
    return (
        updated * lax.rsqrt(row_power / (updated.shape[1] * lax.axis_size("lane")) + 1e-06)[:, None]
    )


def kernel(
    chips, left_hbm, right_hbm, result_hbm, scale_ref, out_ref, power_ref,
    left, right, helper, result, outgoing, incoming, norm_out, norm_in,
    load_sem, left_send, left_recv, right_sem, helper_sem, up_sem, down_sem, across_sem,
    relay_sem, peer_send, peer_recv, part_send, part_recv, norm_send, norm_recv,
):
    band, lane = lax.axis_index("band"), lax.axis_index("lane")
    z, core = band // 2, band % 2
    y, x = lane // 2, lane % 2
    peer = (2 * z + 1 - core, lane)
    lane_x, lane_y, lane_d = 2 * y + 1 - x, 2 * (1 - y) + x, 2 * (1 - y) + 1 - x
    role = z * (1 - y) + (chips - 1 - z) * y
    above, below = (band + 2 - 4 * y, lane), (band - 2 + 4 * y, lane)
    across = (band, lane_y)
    rows, share = left_hbm.shape
    depth, width = right_hbm.shape
    piece = depth // PIECES
    chunk = rows // CHUNKS
    own_at = pl.multiple_of((x + y) % 2 * share, share)
    other_at = pl.multiple_of((x + y + 1) % 2 * share, share)

    def span(at):
        return pl.ds(pl.multiple_of(at * chunk, chunk), chunk)

    load_left = pltpu.make_async_copy(left_hbm, left.at[:, pl.ds(own_at, share)], load_sem.at[0])
    load_left.start()
    load_result = pltpu.make_async_copy(result_hbm, result, load_sem.at[1])

    barrier = pltpu.get_barrier_semaphore()
    for other in (lane_x, lane_y, lane_d):
        pl.semaphore_signal(barrier, inc=1, device_id=(band, other), device_id_type=MESH)
    pl.semaphore_signal(barrier, inc=1, device_id=peer, device_id_type=MESH)

    @pl.when(role < chips - 1)
    def _():
        pl.semaphore_signal(barrier, inc=1, device_id=above, device_id_type=MESH)

    @pl.when(role > 0)
    def _():
        pl.semaphore_signal(barrier, inc=1, device_id=below, device_id_type=MESH)

    pl.semaphore_wait(barrier, 4 + (role + chips - 1) // chips + (2 * chips - 2 - role) // chips)

    def left_copy(at):
        return pltpu.make_async_remote_copy(
            left_hbm.at[span(at), :], left.at[span(at), pl.ds(own_at, share)],
            left_send.at[at], left_recv.at[at], device_id=(band, lane_x), device_id_type=MESH,
        )

    def left_arrival(at):
        return pltpu.make_async_remote_copy(
            left_hbm.at[span(at), :], left.at[span(at), pl.ds(other_at, share)],
            left_send.at[at], left_recv.at[at], device_id=(band, lane_x), device_id_type=MESH,
        )

    def place(slot, part, of_core):
        start = pl.multiple_of((slot % 2 * 2 + of_core) * depth + part * piece, piece)
        return right.at[slot // 2, pl.ds(start, piece), :]

    def own_piece(part):
        return right_hbm.at[pl.ds(part * piece, piece), :]

    def send(of_role, item, part, way):
        if item == "-D":
            slot, source = (D0, D1, X1, X0)[of_role], own_piece(part)
        elif item == "H":
            slot, source = X0, helper.at[part]
        else:
            slot = X1 if item == "-X1" else item
            source = place(slot, part, core)
        at = slot * PIECES + part
        if way == "y":
            target, there, gone = place(slot, part, core), across, across_sem.at[part]
        elif way == "d" and (item == "H" or of_role == 3):
            target, there, gone = helper.at[part], below, relay_sem.at[part]
        elif way == "d":
            target, there, gone = place(slot, part, core), below, down_sem.at[at]
        else:
            target, there, gone = place(slot, part, core), above, up_sem.at[at]
        relayed = way == "d" and (item == "H" or of_role == 3)
        came = helper_sem.at[part] if relayed else right_sem.at[at]
        return pltpu.make_async_remote_copy(
            source, target, gone, came, device_id=there, device_id_type=MESH
        )

    def local_copy(slot, part):
        return pltpu.make_async_copy(
            own_piece(part), place(slot, part, core), right_sem.at[slot * PIECES + part]
        )

    def to_peer(slot, part, of_core):
        at = slot * PIECES + part
        ref = place(slot, part, of_core)
        return pltpu.make_async_remote_copy(
            ref, ref, peer_send.at[at], peer_recv.at[at], device_id=peer, device_id_type=MESH
        )

    def arrival(item, part):
        if item == "H":
            ref, came = helper.at[part], helper_sem.at[part]
        else:
            ref, came = place(item, part, core), right_sem.at[item * PIECES + part]
        return pltpu.make_async_remote_copy(
            ref, ref, came, came, device_id=peer, device_id_type=MESH
        )

    def take(of_role, steps):
        for item, part, ways in steps:
            if item in (X0, X1, D0, D1, "H"):
                arrival(item, part).wait_recv()
            for way in ways:
                send(of_role, item, part, way).start()
            if item in (X0, X1, D0, D1):
                to_peer(item, part, core).start()

    def by_role(table):
        for of_role in range(4):
            if table[of_role]:
                @pl.when(role == of_role)
                def _():
                    take(of_role, table[of_role])

    def await_peer(which):
        for slot in (2 * which, 2 * which + 1):
            for part in range(PIECES):
                to_peer(slot, part, 1 - core).wait_recv()

    def scale(at, start, of_lane):
        factor = scale_ref[:, pl.ds(pl.multiple_of(of_lane * share, share), share)]
        window = left.at[span(at), pl.ds(start, share)]
        window[...] = (window[...].astype(jnp.float32) * factor).astype(jnp.bfloat16)

    def take_left(at):
        left_arrival(at).wait_recv()
        scale(at, other_at, lane_x)

    def product(which, at):
        return jnp.dot(left[span(at), :], right[which], preferred_element_type=jnp.float32)

    def part_copy(at):
        return pltpu.make_async_remote_copy(
            outgoing.at[span(at), :], incoming.at[span(at), :], part_send.at[at],
            part_recv.at[at], device_id=across, device_id_type=MESH,
        )

    def send_part(at):
        outgoing[span(at), :] = product(0, at).astype(jnp.bfloat16)
        part_copy(at).start()

    def keep_part(at):
        out_ref[span(at), :] = result[span(at), :] - product(1, at)

    def finish(at):
        part_copy(at).wait_recv()
        updated = out_ref[span(at), :] - incoming[span(at), :].astype(jnp.float32)
        out_ref[span(at), :] = updated
        power = updated * updated
        power = sum(power[:, k : k + 128] for k in range(0, width, 128))
        norm_out[:, span(at)] = jnp.sum(power.T.reshape(16, 8, chunk), axis=0)

    last = CHUNKS - 1
    groups = (pl.ds(0, last * chunk), pl.ds(last * chunk, chunk))

    def norm_copy(group, k, other):
        return pltpu.make_async_remote_copy(
            norm_out.at[:, groups[group]], norm_in.at[k, :, groups[group]],
            norm_send.at[group, k], norm_recv.at[group, k],
            device_id=(band, other), device_id_type=MESH,
        )

    def norms(group):
        return [norm_copy(group, k, other) for k, other in enumerate((lane_x, lane_y, lane_d))]

    def total(group):
        for copy in norms(group):
            copy.wait_recv()
        at = groups[group]
        power = norm_out[:, at] + norm_in[0, :, at] + norm_in[1, :, at] + norm_in[2, :, at]
        power = jnp.sum(power, axis=0, keepdims=True)
        power_ref[at, :] = jnp.broadcast_to(power, (128, at.size)).T

    by_role(FIRST)
    for at in range(CHUNKS):
        left_copy(at).start()
    load_result.start()

    @pl.when(role == 0)
    def _():
        for part in range(PIECES):
            local_copy(D0, part).start()

    @pl.when(role == 1)
    def _():
        for part in range(PIECES):
            local_copy(D1, part).start()

    load_left.wait()
    pl.loop(0, CHUNKS)(lambda at: scale(at, own_at, lane))

    ready = 4
    for at in range(ready):
        by_role(STEPS[at])
        take_left(at)
    await_peer(0)
    pl.loop(0, ready)(send_part)
    for at in range(ready, last):
        by_role(STEPS[at])
        take_left(at)
        send_part(at)
    await_peer(1)
    load_result.wait()
    pl.loop(0, last)(keep_part)
    take_left(last)
    send_part(last)
    pl.loop(0, last)(finish)
    for copy in norms(0):
        copy.start()
    keep_part(last)
    finish(last)
    for copy in norms(1):
        copy.start()
    total(0)

    for at in range(CHUNKS):
        left_copy(at).wait_send()
        part_copy(at).wait_send()
    for of_role in range(4):
        @pl.when(role == of_role)
        def _():
            for table in (FIRST,) + STEPS:
                for item, part, ways in table[of_role]:
                    for way in ways:
                        send(of_role, item, part, way).wait_send()
    for slot in range(4):
        for part in range(PIECES):
            to_peer(slot, part, core).wait_send()
    total(1)
    for group in range(2):
        for copy in norms(group):
            copy.wait_send()


def on_device(chips, first_factor, second_factor, result_in, pivot_scale):
    rows, share = first_factor.shape
    depth, width = second_factor.shape
    slots = 4 * PIECES
    dma = pltpu.SemaphoreType.DMA
    flops = 2 * rows * share * 4 * width
    updated, power = pl.pallas_call(
        functools.partial(kernel, chips),
        out_shape=(
            jax.ShapeDtypeStruct((rows, width), jnp.float32),
            jax.ShapeDtypeStruct((rows, 128), jnp.float32),
        ),
        in_specs=[
            pl.BlockSpec(memory_space=pltpu.HBM),
            pl.BlockSpec(memory_space=pltpu.HBM),
            pl.BlockSpec(memory_space=pltpu.HBM),
            pl.BlockSpec(memory_space=pltpu.VMEM),
        ],
        out_specs=[pl.BlockSpec(memory_space=pltpu.VMEM)] * 2,
        scratch_shapes=[
            pltpu.VMEM((rows, 2 * share), jnp.bfloat16),
            pltpu.VMEM((2, 4 * depth, width), jnp.bfloat16),
            pltpu.VMEM((PIECES, depth // PIECES, width), jnp.bfloat16),
            pltpu.VMEM((rows, width), jnp.float32),
            pltpu.VMEM((rows, width), jnp.bfloat16),
            pltpu.VMEM((rows, width), jnp.bfloat16),
            pltpu.VMEM((8, rows), jnp.float32),
            pltpu.VMEM((3, 8, rows), jnp.float32),
            dma((2,)),
            dma((CHUNKS,)),
            dma((CHUNKS,)),
            dma((slots,)),
            dma((PIECES,)),
            dma((slots,)),
            dma((slots,)),
            dma((PIECES,)),
            dma((PIECES,)),
            dma((slots,)),
            dma((slots,)),
            dma((CHUNKS,)),
            dma((CHUNKS,)),
            dma((2, 3)),
            dma((2, 3)),
        ],
        compiler_params=pltpu.CompilerParams(
            collective_id=0, has_side_effects=True, vmem_limit_bytes=62 * 1024 * 1024
        ),
        cost_estimate=pl.CostEstimate(
            flops=flops, bytes_accessed=8 * rows * share, transcendentals=0
        ),
    )(first_factor, second_factor, result_in, pivot_scale.reshape(1, -1))
    return updated * lax.rsqrt(power[:, :1] / (width * lax.axis_size("lane")) + 1e-06)


def solution(mesh):
    bands, lanes = mesh.shape["band"], mesh.shape["lane"]

    def body(first_factor, second_factor, result_in, pivot_scale):
        fits = lanes == 4 and bands == 2 * lanes
        plan = functools.partial(on_device, bands // 2) if fits else gathered
        return plan(first_factor, second_factor, result_in, pivot_scale)

    return jax.shard_map(
        body,
        mesh=mesh,
        in_specs=(P("band", "lane"), P("band", "lane"), P("band", "lane"), P()),
        out_specs=P("band", "lane"),
        check_vma=False,
    )
```

time: 80.7 us -> 72.4 us (0.90)
  Pallas kernels: 75.4 us -> 67.8 us
  local copies, waits for them, and re-layouts: 3.35 us -> 0 us
  other arithmetic: 1.74 us -> 4.37 us
    pallas_call x1, Pallas kernels: 75.4 us -> 67.8 us  [on_device(): pl.pallas_call(functools.partial(kernel, chips), out_shape=(jax.ShapeDtyp...]
    unnamed x6 -> x0, local copies, waits for them, and re-layouts: 3.35 us -> none
    mul x1, other arithmetic: 1.52 us -> 3.11 us  [on_device(): updated * lax.rsqrt(power[:, :1] / (width * lax.axis_size('lane')) + 1e-06)]
    rsqrt x1, other arithmetic: 0.22 us -> 1.26 us  [on_device(): lax.rsqrt(power[:, :1] / (width * lax.axis_size('lane')) + 1e-06)]
where the time goes in v1:
time: 72.4 us; the launch traced here: 72.2 us
  Pallas kernels  67.8 us (94%)
  other arithmetic  4.37 us (6%)
    pallas_call x1, Pallas kernels, on_device(): pl.pallas_call(functools.partial(kernel, chips), out_shape=(jax.ShapeDtyp...  67.8 us
    mul x1, other arithmetic, on_device(): updated * lax.rsqrt(power[:, :1] / (width * lax.axis_size('lane')) + 1e-06)  3.11 us

profile of v1, /device:TPU:0, one launch (start us, length us, event | category | flops | bytes accessed | tf_op | source)
XLA Modules:
  0.0 72.2 jit_solution(5072637047441469805)
XLA Ops:
  0.0 67.8 %shard_map.46 = (f32[1024,512]{1,0:T(8,128)}, f32[1024,128]{1,0:T(8,128)}) custom-call(bf16[1024,1024]{1,0:T(8,128)(2,1)} %left_hbm.1, bf16[512,512]{1,0:T(8,128)(2,1)} %right_hbm.1, f32[1024,512]{1,0:T(8,128)} %result_hbm.1, f32[1,4096]{1,0:T(1,128)} %bitcast.1), custom_call_target="tpu_custom_call" | custom-call | flops 4294967296 | bytes 8388608 | tf_op jit(solution)/shard_map/pallas_call | solution.py:333
  67.8 1.3 %rsqrt_reduce_fusion = f32[1024]{0:T(1024)S(1)} fusion(f32[1024,128]{1,0:T(8,128)} %get-tuple-element.8), kind=kLoop, calls=%fused_computation.1 | loop fusion | flops 2048 | bytes 8192 | tf_op jit(solution)/shard_map/rsqrt | solution.py:378
  69.1 3.1 %broadcast_multiply_fusion = f32[1024,512]{1,0:T(8,128)} fusion(f32[1024,512]{1,0:T(8,128)} %get-tuple-element.7, f32[1024]{0:T(1024)S(1)} %rsqrt_reduce_fusion), kind=kLoop, calls=%fused_computation | loop fusion | flops 524288 | bytes 4198400 | tf_op jit(solution)/shard_map/mul | solution.py:378

commit v2 on v1

v2 whole, which is shorter than its diff:
```python
import functools
import heapq

import jax
import jax.numpy as jnp
from jax import lax
from jax.experimental import pallas as pl
from jax.experimental.pallas import tpu as pltpu
from jax.sharding import PartitionSpec as P

MESH = pl.DeviceIdType.MESH
PIECES = 8
CHUNKS = 8
TAIL = (64, 32, 32)
FIRST, SECOND = 2, 3
X0, X1, D0, D1, H = 0, 1, 2, 3, 4
START, BLOCK, HOP = 3.3, 11.6, 2.4


def route():
    half = PIECES // 2
    rank = {X0: 0, H: 0, X1: 1, D1: 4, D0: 5}

    def urgency(item, part):
        return rank[item] + (2 * (part // half) if item not in (D0, D1) else 0)

    here, queued, busy, order, events = {}, {}, {}, {}, []

    def push(when, kind, *what):
        heapq.heappush(events, (when, len(events), kind, what))

    def send(role, way, item, part, lands, when):
        link = (role, way)
        queued.setdefault(link, []).append((urgency(item, part), part, item, lands))
        push(when, "free", link)

    for part in range(PIECES):
        for role, item in ((0, D0), (1, D1), (3, H)):
            push(START, "land", role, item, part)
        send(2, "y", X1, part, (1, X1), START)
        send(3, "y", X0, part, (0, X0), START)
    while events:
        when, _, kind, what = heapq.heappop(events)
        if kind == "free":
            (link,) = what
            if busy.get(link, 0.0) > when + 1e-9 or not queued.get(link):
                continue
            queued[link].sort()
            _, part, item, (role, becomes) = queued[link].pop(0)
            order.setdefault(link, []).append((item, part))
            busy[link] = when + BLOCK / PIECES
            push(busy[link], "free", link)
            push(busy[link] + HOP, "land", role, becomes, part)
            continue
        role, item, part = what
        here[role, item, part] = when
        if item == H:
            if role > 1 or (role == 1 and part % half):
                send(role, "d", H, part, (role - 1, H), when)
            if role < 2:
                send(role, "y", H, part, (2 if role == 1 else 3, X0), when)
        elif role == 1 and item in (X1, D1):
            send(role, "d", item, part, (0, item), when)
        if (
            (item == D0 and role < 3)
            or (item in (X1, D1) and role in (1, 2))
            or (item == X0 and (role == 0 or (role == 2 and part % half == 0)))
        ):
            send(role, "u", item, part, (role + 1, item), when)
    plans = [[], [], [], []]
    for (role, item, part), when in here.items():
        if (role, item) != (3, H):
            plans[role].append((max(when, START + 1.0), -1, "wait", item, part))
    for (role, way), sends in order.items():
        issued = START
        for index, (item, part) in enumerate(sends):
            if role < 2 or way != "y":
                issued = max(issued, here[role, item, part])
            plans[role].append((issued, index, way, item, part))
    return [sorted(plan) for plan in plans]


def gathered(first_factor, second_factor, result_in, pivot_scale):
    share = first_factor.shape[1]
    part_scale = lax.dynamic_slice_in_dim(pivot_scale, lax.axis_index("lane") * share, share)
    scaled_left = (first_factor.astype(jnp.float32) * part_scale).astype(jnp.bfloat16)
    left_line = lax.all_gather(scaled_left, "lane", axis=1, tiled=True)
    right = lax.all_gather(second_factor, "band", axis=0, tiled=True)
    updated = result_in - jnp.dot(left_line, right, preferred_element_type=jnp.float32)
    row_power = lax.psum(jnp.sum(updated * updated, axis=1), "lane")
    return (
        updated * lax.rsqrt(row_power / (updated.shape[1] * lax.axis_size("lane")) + 1e-06)[:, None]
    )


def kernel(
    chips, left_hbm, right_hbm, result_hbm, scale_hbm, out_hbm,
    left, right, helper, result, factors, outgoing, incoming, norm_out, norm_in,
    load_sem, left_send, left_recv, right_sem, helper_sem, way_sem, peer_send, peer_recv,
    part_send, part_recv, norm_send, norm_recv, out_sem,
):
    band, lane = lax.axis_index("band"), lax.axis_index("lane")
    z, core = band // 2, band % 2
    y, x = lane // 2, lane % 2
    peer = (2 * z + 1 - core, lane)
    lane_x, lane_y, lane_d = 2 * y + 1 - x, 2 * (1 - y) + x, 2 * (1 - y) + 1 - x
    role = z * (1 - y) + (chips - 1 - z) * y
    above, below = (band + 2 - 4 * y, lane), (band - 2 + 4 * y, lane)
    across = (band, lane_y)
    rows, share = left_hbm.shape
    lanes = 4
    depth, width = right_hbm.shape
    half = PIECES // 2
    piece, wide = depth // half, width // 2
    chunk = rows // CHUNKS
    own_at = pl.multiple_of((x + y) % 2 * share, share)
    other_at = pl.multiple_of((x + y + 1) % 2 * share, share)

    last = CHUNKS - 1
    sizes = (chunk,) * last + TAIL
    begins = [sum(sizes[:at]) for at in range(len(sizes) + 1)]

    def span(at):
        if isinstance(at, int):
            return pl.ds(begins[at], sizes[at])
        return pl.ds(pl.multiple_of(at * chunk, chunk), chunk)

    load_left = pltpu.make_async_copy(left_hbm, left.at[:, pl.ds(own_at, share)], load_sem.at[0])
    load_left.start()
    load_factors = pltpu.make_async_copy(scale_hbm, factors, load_sem.at[2])
    load_factors.start()
    load_result = pltpu.make_async_copy(result_hbm, result, load_sem.at[1])

    barrier = pltpu.get_barrier_semaphore()
    for other in (lane_x, lane_y, lane_d):
        pl.semaphore_signal(barrier, inc=1, device_id=(band, other), device_id_type=MESH)
    pl.semaphore_signal(barrier, inc=1, device_id=peer, device_id_type=MESH)

    @pl.when(role < chips - 1)
    def _():
        pl.semaphore_signal(barrier, inc=1, device_id=above, device_id_type=MESH)

    @pl.when(role > 0)
    def _():
        pl.semaphore_signal(barrier, inc=1, device_id=below, device_id_type=MESH)

    pl.semaphore_wait(barrier, 4 + (role + chips - 1) // chips + (2 * chips - 2 - role) // chips)

    def left_copy(at):
        return pltpu.make_async_remote_copy(
            left_hbm.at[span(at), :], left.at[span(at), pl.ds(own_at, share)],
            left_send.at[0], left_recv.at[at], device_id=(band, lane_x), device_id_type=MESH,
        )

    def left_arrival(at):
        return pltpu.make_async_remote_copy(
            left_hbm.at[span(at), :], left.at[span(at), pl.ds(other_at, share)],
            left_send.at[0], left_recv.at[at], device_id=(band, lane_x), device_id_type=MESH,
        )

    def place(slot, part, of_core):
        start = (slot % 2 * 2 + of_core) * depth + part % half * piece
        return right.at[
            slot // 2 * 2 + part // half, pl.ds(pl.multiple_of(start, piece), piece), :
        ]

    def own_piece(part):
        return right_hbm.at[
            pl.ds(part % half * piece, piece), pl.ds(part // half * wide, wide)
        ]

    def send(of_role, way, item, part):
        slot = X0 if item == H else item
        at = slot * PIECES + part
        if slot == of_role + D0 or (of_role, way) == (2, "y") or of_role == 3:
            source = own_piece(part)
        else:
            source = helper.at[part] if item == H else place(slot, part, core)
        target, came = place(slot, part, core), right_sem.at[at]
        there, gone = {"u": above, "d": below, "y": across}[way], way_sem.at["udy".index(way)]
        if item == H and way == "d":
            target, came = helper.at[part], helper_sem.at[part]
        return pltpu.make_async_remote_copy(
            source, target, gone, came, device_id=there, device_id_type=MESH
        )

    def local_copy(slot, part):
        return pltpu.make_async_copy(
            own_piece(part), place(slot, part, core), right_sem.at[slot * PIECES + part]
        )

    def to_peer(slot, part, of_core):
        group = slot if slot // 2 else part // half
        ref = place(slot, part, of_core)
        return pltpu.make_async_remote_copy(
            ref, ref, peer_send.at[0], peer_recv.at[group], device_id=peer, device_id_type=MESH
        )

    def await_bytes(ref, semaphore):
        pltpu.make_async_copy(ref, ref, semaphore).wait()

    def await_pieces(count, semaphore):
        blocks = 4 if count % 4 == 0 else 2
        await_bytes(right.at[pl.ds(0, blocks), pl.ds(0, count // blocks * piece), :], semaphore)

    def arrival(item, part):
        if item == H:
            ref, came = helper.at[part], helper_sem.at[part]
        else:
            ref, came = place(item, part, core), right_sem.at[item * PIECES + part]
        return pltpu.make_async_remote_copy(
            ref, ref, came, came, device_id=peer, device_id_type=MESH
        )

    plans = route()

    reach = [
        [
            max(when for when, _, way, item, part in plan if way == "wait" and wanted(item, part))
            for wanted in (
                lambda item, part: item in (X0, X1) and part < half,
                lambda item, part: item in (X0, X1),
                lambda item, part: item == D1,
                lambda item, part: item in (D0, D1),
            )
        ]
        for plan in plans
    ]
    taken = [0.0] * 4

    def take(until, needs=((),) * 4):
        for of_role in range(4):
            due = max([until] + [reach[of_role][need] for need in needs[of_role]])
            steps = [step for step in plans[of_role] if taken[of_role] < step[0] <= due]
            taken[of_role] = due
            if not steps:
                continue

            @pl.when(role == of_role)
            def _():
                for _, _, way, item, part in steps:
                    if way != "wait":
                        send(of_role, way, item, part).start()
                        continue
                    arrival(item, part).wait_recv()
                    if item != H:
                        to_peer(item, part, core).start()

    def await_peer(group):
        await_pieces(PIECES, peer_recv.at[group])

    def scale(at, start, of_lane):
        factor = factors[:, pl.ds(pl.multiple_of(of_lane * share, share), share)]
        window = left.at[span(at), pl.ds(start, share)]
        window[...] = (window[...].astype(jnp.float32) * factor).astype(jnp.bfloat16)

    def take_left(at):
        left_arrival(at).wait_recv()
        scale(at, other_at, lane_x)

    def part_copy(side, at):
        return pltpu.make_async_remote_copy(
            outgoing.at[side, span(at), :], incoming.at[side, span(at), :],
            part_send.at[0], part_recv.at[(at >= last) * 1 if isinstance(at, int) else 0],
            device_id=across, device_id_type=MESH,
        )

    def send_part(side, at):
        part = jnp.dot(left[span(at), :], right[side], preferred_element_type=jnp.float32)
        outgoing[side, span(at), :] = part.astype(jnp.bfloat16)
        part_copy(side, at).start()

    def rows_of(at):
        return pl.ds(pl.multiple_of(at * chunk, chunk), chunk)

    def keep(block, at):
        inner = pl.ds(block * share, share)
        for side in range(2):
            columns = slice(side * wide, (side + 1) * wide)
            result[rows_of(at), columns] = result[rows_of(at), columns] - jnp.dot(
                left[rows_of(at), inner], right[2 + side, inner, :],
                preferred_element_type=jnp.float32,
            )

    def finish(at):
        power = jnp.zeros((chunk, 128), jnp.float32)
        for side in range(2):
            columns = slice(side * wide, (side + 1) * wide)
            updated = result[rows_of(at), columns] - incoming[side, rows_of(at), :].astype(
                jnp.float32
            )
            result[rows_of(at), columns] = updated
            for k in range(0, wide, 128):
                power += updated[:, k : k + 128] * updated[:, k : k + 128]
        norm_out[:, rows_of(at)] = jnp.sum(power.T.reshape(16, 8, chunk), axis=0)

    def norms(group):
        rows_at = pl.ds(group * last * chunk, chunk if group else last * chunk)
        return [
            pltpu.make_async_remote_copy(
                norm_out.at[:, rows_at], norm_in.at[k, :, rows_at],
                norm_send.at[0], norm_recv.at[group],
                device_id=(band, other), device_id_type=MESH,
            )
            for k, other in enumerate((lane_x, lane_y, lane_d))
        ]

    def out_copy(group):
        rows_at = pl.ds(group * last * chunk, chunk if group else last * chunk)
        return pltpu.make_async_copy(
            result.at[rows_at, :], out_hbm.at[rows_at, :], out_sem.at[group]
        )

    def rescale(at):
        power = norm_out[:, rows_of(at)]
        for k in range(3):
            power = power + norm_in[k, :, rows_of(at)]
        power = jnp.sum(power, axis=0, keepdims=True)
        factor = lax.rsqrt(power / (width * lanes) + 1e-06)
        factor = jnp.broadcast_to(factor, (128, chunk)).T
        for k in range(0, width, 128):
            result[rows_of(at), k : k + 128] = result[rows_of(at), k : k + 128] * factor

    scope = jax.named_scope
    for at in range(len(sizes)):
        left_copy(at).start()
    take(START)

    @pl.when(role == 0)
    def _():
        for part in range(PIECES):
            local_copy(D0, part).start()

    @pl.when(role == 1)
    def _():
        for part in range(PIECES):
            local_copy(D1, part).start()

    load_result.start()
    with scope("own"):
        load_factors.wait()
        load_left.wait()
        pl.loop(0, CHUNKS)(lambda at: scale(at, own_at, lane))

    def keep_most():
        with scope("await_d0"):
            await_peer(D0)
        with scope("keep_d0"):
            pl.loop(0, last - 1)(lambda i: keep(0, i))

    needed = {
        FIRST: ((0,),) * 4,
        SECOND: ((1,),) * 4,
        last - 2: ((2, 3), (2, 3), (2,), (2,)),
        last - 1: ((), (), (3,), ()),
        len(sizes) - 1: ((), (), (), (3,)),
    }
    for at in range(len(sizes)):
        due = START + 4 * BLOCK * begins[at + 1] / rows + 0.7
        with scope(f"take{at}"):
            take(due, needed.get(at, ((),) * 4))
        with scope(f"left{at}"):
            left_arrival(at).wait_recv()
        with scope(f"scale{at}"):
            scale(at, other_at, lane_x)
        for side, ready in ((0, FIRST), (1, SECOND)):
            if at == ready:
                with scope(f"await_x{side}"):
                    await_peer(side)
                with scope(f"parts{side}"):
                    pl.loop(0, ready + 1)(lambda i: send_part(side, i))
            elif at > ready:
                with scope(f"part{side}_{at}"):
                    send_part(side, at)
        if at == last - 2:
            with scope("await_d1"):
                await_peer(D1)
                load_result.wait()
            with scope("keep_d1"):
                pl.loop(0, last - 1)(lambda i: keep(1, i))
            pl.when(role < 2)(keep_most)
        if at == last - 1:
            pl.when(role == 2)(keep_most)
    pl.when(role == 3)(keep_most)
    with scope("keep_rest"):
        for at in range(last - 1, CHUNKS):
            keep(1, at)
            keep(0, at)
    with scope("await_parts"):
        await_bytes(incoming.at[:, pl.ds(0, last * chunk), :], part_recv.at[0])
    with scope("finish"):
        pl.loop(0, last)(finish)
        for copy in norms(0):
            copy.start()
    with scope("await_tail"):
        await_bytes(incoming.at[:, pl.ds(last * chunk, chunk), :], part_recv.at[1])
    with scope("finish_tail"):
        finish(last)
        for copy in norms(1):
            copy.start()
    with scope("await_norm0"):
        await_bytes(norm_in.at[:, :, pl.ds(0, last * chunk)], norm_recv.at[0])
    with scope("rescale0"):
        pl.loop(0, last)(rescale)
        out_copy(0).start()
    with scope("await_norm1"):
        await_bytes(norm_in.at[:, :, pl.ds(last * chunk, chunk)], norm_recv.at[1])
    with scope("rescale1"):
        rescale(last)
        out_copy(1).start()

    with scope("sends"):
        await_bytes(left_hbm, left_send.at[0])
        await_bytes(outgoing, part_send.at[0])
        await_bytes(norm_in, norm_send.at[0])
        await_pieces(4 * PIECES, peer_send.at[0])
        for of_role in range(4):
            @pl.when(role == of_role)
            def _():
                for index, way in enumerate("udy"):
                    count = sum(step[2] == way for step in plans[of_role])
                    if count:
                        await_pieces(count, way_sem.at[index])
    with scope("out"):
        for group in range(2):
            out_copy(group).wait()


def on_device(chips, first_factor, second_factor, result_in, pivot_scale):
    rows, share = first_factor.shape
    depth, width = second_factor.shape
    slots, parts = 4 * PIECES, CHUNKS - 1 + len(TAIL)
    dma = pltpu.SemaphoreType.DMA
    flops = 2 * rows * share * 4 * width
    return pl.pallas_call(
        functools.partial(kernel, chips),
        out_shape=pltpu.VMEM((rows, width), jnp.float32),
        in_specs=[
            pl.BlockSpec(memory_space=pltpu.HBM),
            pl.BlockSpec(memory_space=pltpu.HBM),
            pl.BlockSpec(memory_space=pltpu.HBM),
            pl.BlockSpec(memory_space=pltpu.HBM),
        ],
        out_specs=pl.BlockSpec(memory_space=pl.ANY),
        scratch_shapes=[
            pltpu.VMEM((rows, 2 * share), jnp.bfloat16),
            pltpu.VMEM((4, 4 * depth, width // 2), jnp.bfloat16),
            pltpu.VMEM((PIECES, 2 * depth // PIECES, width // 2), jnp.bfloat16),
            pltpu.VMEM((rows, width), jnp.float32),
            pltpu.VMEM((1, 4 * share), jnp.float32),
            pltpu.VMEM((2, rows, width // 2), jnp.bfloat16),
            pltpu.VMEM((2, rows, width // 2), jnp.bfloat16),
            pltpu.VMEM((8, rows), jnp.float32),
            pltpu.VMEM((3, 8, rows), jnp.float32),
            dma((3,)),
            dma((1,)),
            dma((parts,)),
            dma((slots,)),
            dma((PIECES,)),
            dma((3,)),
            dma((1,)),
            dma((4,)),
            dma((1,)),
            dma((2,)),
            dma((1,)),
            dma((2,)),
            dma((2,)),
        ],
        compiler_params=pltpu.CompilerParams(
            collective_id=0, has_side_effects=True, vmem_limit_bytes=56 * 1024 * 1024
        ),
        cost_estimate=pl.CostEstimate(
            flops=flops, bytes_accessed=8 * rows * share, transcendentals=0
        ),
    )(first_factor, second_factor, result_in, pivot_scale.reshape(1, -1))


def solution(mesh):
    bands, lanes = mesh.shape["band"], mesh.shape["lane"]

    def body(first_factor, second_factor, result_in, pivot_scale):
        fits = lanes == 4 and bands == 2 * lanes
        plan = functools.partial(on_device, bands // 2) if fits else gathered
        return plan(first_factor, second_factor, result_in, pivot_scale)

    return jax.shard_map(
        body,
        mesh=mesh,
        in_specs=(P("band", "lane"), P("band", "lane"), P("band", "lane"), P()),
        out_specs=P("band", "lane"),
        check_vma=False,
    )
```

time: 72.4 us -> 61.3 us (0.85)
  Pallas kernels: 67.8 us -> 59.8 us
  other arithmetic: 4.37 us -> 0 us
  local copies, waits for them, and re-layouts: 0 us -> 1.32 us
    pallas_call x1, Pallas kernels: 67.8 us -> 59.8 us  [on_device(): pl.pallas_call(functools.partial(kernel, chips), out_shape=pltpu.VMEM((ro...]
    mul x1 -> x0, other arithmetic: 3.11 us -> none  [on_device(): updated * lax.rsqrt(power[:, :1] / (width * lax.axis_size('lane')) + 1e-06)]
    unnamed x0 -> x1, local copies, waits for them, and re-layouts: none -> 1.32 us
    rsqrt x1 -> x0, other arithmetic: 1.26 us -> none  [on_device(): lax.rsqrt(power[:, :1] / (width * lax.axis_size('lane')) + 1e-06)]
where the time goes in v2:
time: 61.3 us; the launch traced here: 61.1 us
  Pallas kernels  59.8 us (98%)
  local copies, waits for them, and re-layouts  1.32 us (2%)
    pallas_call x1, Pallas kernels, on_device(): pl.pallas_call(functools.partial(kernel, chips), out_shape=pltpu.VMEM((ro...  59.8 us
    unnamed x1, local copies, waits for them, and re-layouts  1.32 us

profile of v2, /device:TPU:0, one launch (start us, length us, event | category | flops | bytes accessed | tf_op | source)
XLA Modules:
  0.0 61.1 jit_solution(10157636734892335656)
XLA Ops:
  0.0 59.8 %shard_map.46 = f32[1024,512]{1,0:T(8,128)S(1)} custom-call(bf16[1024,1024]{1,0:T(8,128)(2,1)} %left_hbm.1, bf16[512,512]{1,0:T(8,128)(2,1)} %right_hbm.1, f32[1024,512]{1,0:T(8,128)} %result_hbm.1, f32[1,4096]{1,0:T(1,128)} %bitcast.1), custom_call_target="tpu_custom_call" | custom-call | flops 4294967296 | bytes 8388608 | tf_op jit(solution)/shard_map/pallas_call | solution.py:435
  59.8 1.3 %copy.6 = f32[1024,512]{1,0:T(8,128)} copy(f32[1024,512]{1,0:T(8,128)S(1)} %shard_map.46) | data formatting | bytes 4194304

commit v3 on v2

--- a/solution.py
+++ b/solution.py
@@ -11,6 +11,7 @@
 MESH = pl.DeviceIdType.MESH
 PIECES = 8
 CHUNKS = 8
+RELAYED = (1, 2, 3, 6, 7)
 TAIL = (64, 32, 32)
 FIRST, SECOND = 2, 3
 X0, X1, D0, D1, H = 0, 1, 2, 3, 4
@@ -55,7 +56,7 @@
         role, item, part = what
         here[role, item, part] = when
         if item == H:
-            if role > 1 or (role == 1 and part % half):
+            if role > 1 or (role == 1 and part in RELAYED):
                 send(role, "d", H, part, (role - 1, H), when)
             if role < 2:
                 send(role, "y", H, part, (2 if role == 1 else 3, X0), when)
@@ -64,7 +65,7 @@
         if (
             (item == D0 and role < 3)
             or (item in (X1, D1) and role in (1, 2))
-            or (item == X0 and (role == 0 or (role == 2 and part % half == 0)))
+            or (item == X0 and (role == 0 or (role == 2 and part not in RELAYED)))
         ):
             send(role, "u", item, part, (role + 1, item), when)
     plans = [[], [], [], []]
@@ -95,7 +96,7 @@
 
 def kernel(
     chips, left_hbm, right_hbm, result_hbm, scale_hbm, out_hbm,
-    left, right, helper, result, factors, outgoing, incoming, norm_out, norm_in,
+    left, right, helper, result, factors, early, outgoing, incoming, norm_out, norm_in,
     load_sem, left_send, left_recv, right_sem, helper_sem, way_sem, peer_send, peer_recv,
     part_send, part_recv, norm_send, norm_recv, out_sem,
 ):
@@ -132,7 +133,7 @@
     load_result = pltpu.make_async_copy(result_hbm, result, load_sem.at[1])
 
     barrier = pltpu.get_barrier_semaphore()
-    for other in (lane_x, lane_y, lane_d):
+    for other in (lane_x, lane_y):
         pl.semaphore_signal(barrier, inc=1, device_id=(band, other), device_id_type=MESH)
     pl.semaphore_signal(barrier, inc=1, device_id=peer, device_id_type=MESH)
 
@@ -144,7 +145,7 @@
     def _():
         pl.semaphore_signal(barrier, inc=1, device_id=below, device_id_type=MESH)
 
-    pl.semaphore_wait(barrier, 4 + (role + chips - 1) // chips + (2 * chips - 2 - role) // chips)
+    pl.semaphore_wait(barrier, 3 + (role + chips - 1) // chips + (2 * chips - 2 - role) // chips)
 
     def left_copy(at):
         return pltpu.make_async_remote_copy(
@@ -190,7 +191,7 @@
         )
 
     def to_peer(slot, part, of_core):
-        group = slot if slot // 2 else part // half
+        group = {X0: 0, X1: 0, D1: 2, D0: 3}[slot] + (slot != D1) * (part // half)
         ref = place(slot, part, of_core)
         return pltpu.make_async_remote_copy(
             ref, ref, peer_send.at[0], peer_recv.at[group], device_id=peer, device_id_type=MESH
@@ -200,7 +201,7 @@
         pltpu.make_async_copy(ref, ref, semaphore).wait()
 
     def await_pieces(count, semaphore):
-        blocks = 4 if count % 4 == 0 else 2
+        blocks = next(k for k in (4, 3, 2, 1) if count % k == 0)
         await_bytes(right.at[pl.ds(0, blocks), pl.ds(0, count // blocks * piece), :], semaphore)
 
     def arrival(item, part):
@@ -221,6 +222,7 @@
                 lambda item, part: item in (X0, X1) and part < half,
                 lambda item, part: item in (X0, X1),
                 lambda item, part: item == D1,
+                lambda item, part: item == D0 and part < half,
                 lambda item, part: item in (D0, D1),
             )
         ]
@@ -232,7 +234,7 @@
         for of_role in range(4):
             due = max([until] + [reach[of_role][need] for need in needs[of_role]])
             steps = [step for step in plans[of_role] if taken[of_role] < step[0] <= due]
-            taken[of_role] = due
+            taken[of_role] = max(due, taken[of_role])
             if not steps:
                 continue
 
@@ -247,7 +249,7 @@
                         to_peer(item, part, core).start()
 
     def await_peer(group):
-        await_pieces(PIECES, peer_recv.at[group])
+        await_pieces(PIECES if group < 3 else half, peer_recv.at[group])
 
     def scale(at, start, of_lane):
         factor = factors[:, pl.ds(pl.multiple_of(of_lane * share, share), share)]
@@ -265,17 +267,26 @@
             device_id=across, device_id_type=MESH,
         )
 
+    def partial(side, rows_at, inner):
+        return jnp.dot(
+            left[rows_at, inner], right[side, inner, :], preferred_element_type=jnp.float32
+        )
+
     def send_part(side, at):
-        part = jnp.dot(left[span(at), :], right[side], preferred_element_type=jnp.float32)
+        if isinstance(at, int) and at >= last:
+            early_at = pl.ds(begins[at] - last * chunk, sizes[at])
+            part = early[side, early_at, :] + partial(side, span(at), pl.ds(other_at, share))
+        else:
+            part = partial(side, span(at), pl.ds(0, 2 * share))
         outgoing[side, span(at), :] = part.astype(jnp.bfloat16)
         part_copy(side, at).start()
 
     def rows_of(at):
         return pl.ds(pl.multiple_of(at * chunk, chunk), chunk)
 
-    def keep(block, at):
+    def keep(block, at, sides=(0, 1)):
         inner = pl.ds(block * share, share)
-        for side in range(2):
+        for side in sides:
             columns = slice(side * wide, (side + 1) * wide)
             result[rows_of(at), columns] = result[rows_of(at), columns] - jnp.dot(
                 left[rows_of(at), inner], right[2 + side, inner, :],
@@ -292,7 +303,7 @@
             result[rows_of(at), columns] = updated
             for k in range(0, wide, 128):
                 power += updated[:, k : k + 128] * updated[:, k : k + 128]
-        norm_out[:, rows_of(at)] = jnp.sum(power.T.reshape(16, 8, chunk), axis=0)
+        norm_out[:, rows_of(at)] = jnp.sum(power.T, axis=0, keepdims=True)
 
     def norms(group):
         rows_at = pl.ds(group * last * chunk, chunk if group else last * chunk)
@@ -315,7 +326,6 @@
         power = norm_out[:, rows_of(at)]
         for k in range(3):
             power = power + norm_in[k, :, rows_of(at)]
-        power = jnp.sum(power, axis=0, keepdims=True)
         factor = lax.rsqrt(power / (width * lanes) + 1e-06)
         factor = jnp.broadcast_to(factor, (128, chunk)).T
         for k in range(0, width, 128):
@@ -342,18 +352,14 @@
         load_left.wait()
         pl.loop(0, CHUNKS)(lambda at: scale(at, own_at, lane))
 
-    def keep_most():
-        with scope("await_d0"):
-            await_peer(D0)
-        with scope("keep_d0"):
-            pl.loop(0, last - 1)(lambda i: keep(0, i))
+    def keep_some(block, begin, end, sides=(0, 1)):
+        with scope(f"keep{block}_{end}_{sides[0]}"):
+            pl.loop(begin, end)(lambda i: keep(block, i, sides))
 
     needed = {
-        FIRST: ((0,),) * 4,
-        SECOND: ((1,),) * 4,
-        last - 2: ((2, 3), (2, 3), (2,), (2,)),
-        last - 1: ((), (), (3,), ()),
-        len(sizes) - 1: ((), (), (), (3,)),
+        last - 2: ((2, 4), (2, 4), (2,), (2,)),
+        last - 1: ((), (), (4,), (3,)),
+        len(sizes) - 1: ((), (), (), (4,)),
     }
     for at in range(len(sizes)):
         due = START + 4 * BLOCK * begins[at + 1] / rows + 0.7
@@ -365,6 +371,7 @@
             scale(at, other_at, lane_x)
         for side, ready in ((0, FIRST), (1, SECOND)):
             if at == ready:
+                take(0.0, ((side,),) * 4)
                 with scope(f"await_x{side}"):
                     await_peer(side)
                 with scope(f"parts{side}"):
@@ -372,26 +379,60 @@
             elif at > ready:
                 with scope(f"part{side}_{at}"):
                     send_part(side, at)
+        if at == SECOND:
+            with scope("early"):
+                for side in range(2):
+                    early[side] = partial(
+                        side, pl.ds(last * chunk, chunk), pl.ds(own_at, share)
+                    )
         if at == last - 2:
             with scope("await_d1"):
-                await_peer(D1)
+                await_peer(2)
                 load_result.wait()
-            with scope("keep_d1"):
-                pl.loop(0, last - 1)(lambda i: keep(1, i))
-            pl.when(role < 2)(keep_most)
+            keep_some(1, 0, last - 1)
+
+            @pl.when(role < 2)
+            def _():
+                await_peer(3)
+                await_peer(4)
+                keep_some(0, 0, last - 1)
         if at == last - 1:
-            pl.when(role == 2)(keep_most)
-    pl.when(role == 3)(keep_most)
-    with scope("keep_rest"):
-        for at in range(last - 1, CHUNKS):
-            keep(1, at)
-            keep(0, at)
+            keep(1, last - 1)
+
+            @pl.when(role < 2)
+            def _():
+                keep(0, last - 1)
+
+            @pl.when(role == 2)
+            def _():
+                await_peer(3)
+                await_peer(4)
+                keep_some(0, 0, 3)
+
+            @pl.when(role == 3)
+            def _():
+                await_peer(3)
+                keep_some(0, 0, last - 1, (0,))
+
+    @pl.when(role == 2)
+    def _():
+        keep_some(0, 3, last)
+
+    @pl.when(role == 3)
+    def _():
+        keep(0, last - 1, (0,))
+        await_peer(4)
+        keep_some(0, 0, last, (1,))
+
     with scope("await_parts"):
         await_bytes(incoming.at[:, pl.ds(0, last * chunk), :], part_recv.at[0])
     with scope("finish"):
-        pl.loop(0, last)(finish)
+        pl.loop(0, last, unroll=True)(finish)
         for copy in norms(0):
             copy.start()
+    with scope("keep_last"):
+        keep(1, last)
+        keep(0, last)
     with scope("await_tail"):
         await_bytes(incoming.at[:, pl.ds(last * chunk, chunk), :], part_recv.at[1])
     with scope("finish_tail"):
@@ -401,7 +442,7 @@
     with scope("await_norm0"):
         await_bytes(norm_in.at[:, :, pl.ds(0, last * chunk)], norm_recv.at[0])
     with scope("rescale0"):
-        pl.loop(0, last)(rescale)
+        pl.loop(0, last, unroll=True)(rescale)
         out_copy(0).start()
     with scope("await_norm1"):
         await_bytes(norm_in.at[:, :, pl.ds(last * chunk, chunk)], norm_recv.at[1])
@@ -448,10 +489,11 @@
             pltpu.VMEM((PIECES, 2 * depth // PIECES, width // 2), jnp.bfloat16),
             pltpu.VMEM((rows, width), jnp.float32),
             pltpu.VMEM((1, 4 * share), jnp.float32),
+            pltpu.VMEM((2, rows // CHUNKS, width // 2), jnp.float32),
             pltpu.VMEM((2, rows, width // 2), jnp.bfloat16),
             pltpu.VMEM((2, rows, width // 2), jnp.bfloat16),
-            pltpu.VMEM((8, rows), jnp.float32),
-            pltpu.VMEM((3, 8, rows), jnp.float32),
+            pltpu.VMEM((1, rows), jnp.float32),
+            pltpu.VMEM((3, 1, rows), jnp.float32),
             dma((3,)),
             dma((1,)),
             dma((parts,)),
@@ -459,7 +501,7 @@
             dma((PIECES,)),
             dma((3,)),
             dma((1,)),
-            dma((4,)),
+            dma((5,)),
             dma((1,)),
             dma((2,)),
             dma((1,)),

time: 61.3 us -> 58.7 us (0.958)
  Pallas kernels: 59.8 us -> 57.2 us
    pallas_call x1, Pallas kernels: 59.8 us -> 57.2 us  [on_device(): pl.pallas_call(functools.partial(kernel, chips), out_shape=pltpu.VMEM((ro...]
where the time goes in v3:
time: 58.7 us; the launch traced here: 58.6 us
  Pallas kernels  57.2 us (97%)
  local copies, waits for them, and re-layouts  1.32 us (2%)
    pallas_call x1, Pallas kernels, on_device(): pl.pallas_call(functools.partial(kernel, chips), out_shape=pltpu.VMEM((ro...  57.2 us
    unnamed x1, local copies, waits for them, and re-layouts  1.32 us

profile of v3, /device:TPU:0, one launch (start us, length us, event | category | flops | bytes accessed | tf_op | source)
XLA Modules:
  0.0 58.6 jit_solution(9330506062522572275)
XLA Ops:
  0.0 57.2 %shard_map.46 = f32[1024,512]{1,0:T(8,128)S(1)} custom-call(bf16[1024,1024]{1,0:T(8,128)(2,1)} %left_hbm.1, bf16[512,512]{1,0:T(8,128)(2,1)} %right_hbm.1, f32[1024,512]{1,0:T(8,128)} %result_hbm.1, f32[1,4096]{1,0:T(1,128)} %bitcast.1), custom_call_target="tpu_custom_call" | custom-call | flops 4294967296 | bytes 8388608 | tf_op jit(solution)/shard_map/pallas_call | solution.py:476
  57.2 1.3 %copy.6 = f32[1024,512]{1,0:T(8,128)} copy(f32[1024,512]{1,0:T(8,128)S(1)} %shard_map.46) | data formatting | bytes 4194304

commit v4 on v3

--- a/solution.py
+++ b/solution.py
@@ -332,8 +332,14 @@
             result[rows_of(at), k : k + 128] = result[rows_of(at), k : k + 128] * factor
 
     scope = jax.named_scope
-    for at in range(len(sizes)):
+    for at in range(last):
         left_copy(at).start()
+
+    @pl.when(core == 0)
+    def _():
+        for at in range(last, len(sizes)):
+            left_copy(at).start()
+
     take(START)
 
     @pl.when(role == 0)
@@ -367,6 +373,13 @@
             take(due, needed.get(at, ((),) * 4))
         with scope(f"left{at}"):
             left_arrival(at).wait_recv()
+        if at == last - 1:
+
+            @pl.when(core == 1)
+            def _():
+                for late in range(last, len(sizes)):
+                    left_copy(late).start()
+
         with scope(f"scale{at}"):
             scale(at, other_at, lane_x)
         for side, ready in ((0, FIRST), (1, SECOND)):

time: 58.7 us -> 58.7 us (level)
  no operation moved by 1% of the time
where the time goes in v4:
time: 58.7 us; the launch traced here: 58.6 us
  Pallas kernels  57.2 us (97%)
  local copies, waits for them, and re-layouts  1.32 us (2%)
    pallas_call x1, Pallas kernels, on_device(): pl.pallas_call(functools.partial(kernel, chips), out_shape=pltpu.VMEM((ro...  57.2 us
    unnamed x1, local copies, waits for them, and re-layouts  1.32 us

profile of v4, /device:TPU:0, one launch (start us, length us, event | category | flops | bytes accessed | tf_op | source)
XLA Modules:
  0.0 58.6 jit_solution(11873615142246682701)
XLA Ops:
  0.0 57.2 %shard_map.46 = f32[1024,512]{1,0:T(8,128)S(1)} custom-call(bf16[1024,1024]{1,0:T(8,128)(2,1)} %left_hbm.1, bf16[512,512]{1,0:T(8,128)(2,1)} %right_hbm.1, f32[1024,512]{1,0:T(8,128)} %result_hbm.1, f32[1,4096]{1,0:T(1,128)} %bitcast.1), custom_call_target="tpu_custom_call" | custom-call | flops 4294967296 | bytes 8388608 | tf_op jit(solution)/shard_map/pallas_call | solution.py:489
  57.2 1.3 %copy.6 = f32[1024,512]{1,0:T(8,128)} copy(f32[1024,512]{1,0:T(8,128)S(1)} %shard_map.46) | data formatting | bytes 4194304
